TPU v7x, 128 devices: a whole 4x4x4 slice. The times are simulated.
128 devices in a mesh: rep: 2 (over core), dp: 64 (over x, y, z).
Axes of the slice: x: 4, y: 4, z: 4, core: 2. Of those that a mesh axis runs over, the one named last changes fastest.
Arguments:
- x: bfloat16 [128, 2048, 896], P(('rep', 'dp')), parts along dimension 0
- dy: bfloat16 [128, 2048, 896], P(('rep', 'dp')), parts along dimension 0
- w_gate: bfloat16 [2, 896, 2304], replicated
- w_up: bfloat16 [2, 896, 2304], replicated
- w_down: bfloat16 [2, 2304, 896], replicated
- m_w_gate: float32 [2, 896, 2304], replicated
- m_w_up: float32 [2, 896, 2304], replicated
- m_w_down: float32 [2, 2304, 896], replicated
- v_w_gate: float32 [2, 896, 2304], replicated
- v_w_up: float32 [2, 896, 2304], replicated
- v_w_down: float32 [2, 2304, 896], replicated
Outputs:
- output 1: bfloat16 [4, 896, 2304], P('rep'), parts along dimension 0
- output 2: bfloat16 [4, 896, 2304], P('rep'), parts along dimension 0
- output 3: bfloat16 [4, 2304, 896], P('rep'), parts along dimension 0
- output 4: float32 [4, 896, 2304], P('rep'), parts along dimension 0
- output 5: float32 [4, 896, 2304], P('rep'), parts along dimension 0
- output 6: float32 [4, 2304, 896], P('rep'), parts along dimension 0
- output 7: float32 [4, 896, 2304], P('rep'), parts along dimension 0
- output 8: float32 [4, 896, 2304], P('rep'), parts along dimension 0
- output 9: float32 [4, 2304, 896], P('rep'), parts along dimension 0
There are 2 independent parts. A program takes and returns all parts, laid end to end along the dimension named above; an argument that names none is the same for every part.
All inputs are finite; a program needn't handle non-finite values.
Results may differ from a plain program's by a relative error of at most 0.022.
Values are sent between devices in bfloat16 or wider.
A program may use at most 1.5 GiB of HBM per device.

v0:
```python
import jax
import jax.numpy as jnp
from jax import lax
from jax.sharding import PartitionSpec as P

NAMES = ("w_gate", "w_up", "w_down")


def matmul(a, w):
    return jnp.dot(a, w, preferred_element_type=jnp.float32).astype(jnp.bfloat16)


def normed(h):
    wide = h.astype(jnp.float32)
    scale = lax.rsqrt(jnp.mean(wide**2, -1, keepdims=True) + 1e-6)
    return (wide * scale).astype(jnp.bfloat16)


def layer(h, w):
    a = normed(h)
    gate = jnp.dot(a, w["w_gate"], preferred_element_type=jnp.float32)
    up = jnp.dot(a, w["w_up"], preferred_element_type=jnp.float32)
    return h + matmul((jax.nn.silu(gate) * up).astype(jnp.bfloat16), w["w_down"])


def adamw(w, m, v, g):
    m = 0.9 * m + 0.1 * g
    v = 0.95 * v + 0.05 * g * g
    step = m * lax.rsqrt(v + 1e-8) + 0.1 * w
    return (w - 0.02 * step).astype(jnp.bfloat16), m, v


def clipped(gradients, sum_of_squares, count):
    factor = jnp.minimum(1.0, 0.5 * lax.rsqrt(sum_of_squares / count + 1e-30))
    return [g * factor for g in gradients]


def solution(mesh):
    def step(x, dy, *arrays):
        weights, m, v = (arrays[i : i + 3] for i in (0, 3, 6))
        layers = weights[0].shape[0]
        h, kept = x[0], []
        for number in range(layers):
            kept.append(h)
            h = layer(h, {name: w[number] for name, w in zip(NAMES, weights, strict=True)})
        by_h, summed = dy[0], [None] * layers
        for number in reversed(range(layers)):
            _, back = jax.vjp(lambda w, h: layer(h, w), {name: w[number] for name, w in zip(NAMES, weights, strict=True)}, kept[number])
            by_w, by_h = back(by_h)
            summed[number] = [lax.psum(by_w[name], "dp") for name in NAMES]
        gradients = [jnp.stack([summed[number][i] for number in range(layers)]).astype(jnp.float32) for i in range(3)]
        gradients = clipped(gradients, sum(jnp.sum(g * g) for g in gradients), sum(g.size for g in gradients))
        new = [adamw(w.astype(jnp.float32), m, v, g) for w, m, v, g in zip(weights, m, v, gradients, strict=True)]
        return tuple(one[which] for which in range(3) for one in new)

    return jax.shard_map(
        step,
        mesh=mesh,
        in_specs=(P(("rep", "dp"), None, None),) * 2 + (P(None, None, None),) * 9,
        out_specs=(P("rep", None, None),) * 9,
        check_vma=False,
    )
```

profile of v0, /device:TPU:0, one launch (start us, length us, event | category | flops | bytes accessed | tf_op | source)
XLA Modules:
  0.0 676.0 jit_solution(3661711657494759910)
XLA Ops:
  7.2 0.0 all-reduce.3.cloned.1.call-start
  7.2 6.1 copy.20
  13.3 2.8 fusion.36
  16.1 6.1 copy.21
  22.3 15.2 %convolution_convert_fusion.1 = bf16[2048,2304]{1,0:T(8,128)(2,1)} fusion(bf16[2,2304,896]{2,1,0:T(8,128)(2,1)} %param.15, bf16[1,2048,896]{2,1,0:T(8,128)(2,1)} %param.12), kind=kOutput, calls=%fused_computation.63 | convolution fusion | flops 8460435456 | bytes 17235968 | tf_op jit(solution)/shard_map/transpose(jvp())/dot_general | solution.py:10
  37.5 15.5 %fusion.70 = f32[2048,2304]{1,0:T(8,128)} fusion(bf16[2,896,2304]{2,1,0:T(8,128)(2,1)} %param.13, bf16[1,2048,896]{2,1,0:T(8,128)(2,1)S(1)} %copy-done.4, f32[2048]{0:T(1024)S(1)} %add_rsqrt_fusion), kind=kOutput, calls=%fused_computation.105 | convolution fusion | flops 8461221888 | bytes 26681344 | tf_op jit(solution)/shard_map/dot_general | solution.py:21
  53.0 21.6 %multiply_convert_fusion.1 = (bf16[2048,2304]{1,0:T(8,128)(2,1)}, f32[2048,2304]{1,0:T(8,128)}) fusion(f32[2048,2304]{1,0:T(8,128)} %fusion.70, bf16[2,896,2304]{2,1,0:T(8,128)(2,1)} %param.14, bf16[1,2048,896]{2,1,0:T(8,128)(2,1)} %param.11, f32[2048]{0:T(1024)S(1)} %add_rsqrt_fusion), kind=kOutput, calls=%fused_computation.35 | convolution fusion | flops 8489533440 | bytes 54992896 | tf_op jit(solution)/shard_map/dot_general | solution.py:22
  74.6 14.1 %fusion.40 = (f32[2048]{0:T(1024)S(1)}, bf16[2048,896]{0,1:T(8,128)(2,1)S(1)}) fusion(bf16[2048,2304]{1,0:T(8,128)(2,1)} %get-tuple-element.24, bf16[2,2304,896]{2,1,0:T(8,128)(2,1)} %param.15, bf16[1,2048,896]{1,2,0:T(8,128)(2,1)} %copy.20), kind=kOutput, calls=%fused_computation.76 | convolution fusion | flops 8464889856 | bytes 20914176 | tf_op jit(solution)/shard_map/dot_general | solution.py:10
  88.7 0.0 copy-start.5
  88.7 0.0 copy-start.8
  88.7 16.3 %fusion.57 = f32[2048,2304]{1,0:T(8,128)} fusion(bf16[2,896,2304]{2,1,0:T(8,128)(2,1)} %param.14, bf16[2048,896]{0,1:T(8,128)(2,1)S(1)} %get-tuple-element.27, f32[2048]{0:T(1024)S(1)} %fusion.98), kind=kOutput, calls=%fused_computation.92 | convolution fusion | flops 8461221888 | bytes 26681344 | tf_op jit(solution)/shard_map/jvp()/dot_general | solution.py:22
  105.1 26.3 %fusion.5 = (bf16[2048,2304]{1,0:T(8,128)(2,1)}, f32[2048,2304]{1,0:T(8,128)}) fusion(f32[2048,2304]{1,0:T(8,128)} %fusion.57, bf16[2048,2304]{1,0:T(8,128)(2,1)} %convolution_convert_fusion.1, bf16[2,896,2304]{2,1,0:T(8,128)(2,1)} %param.13, bf16[2048,896]{0,1:T(8,128)(2,1)S(1)} %get-tuple-element.27, f32[2048]{0:T(1024)S(1)} %fusion.98), kind=kOutput, calls=%fused_computation.26 | convolution fusion | flops 8517844992 | bytes 64430080 | tf_op jit(solution)/shard_map/jvp()/dot_general | solution.py:21
  131.4 16.8 %fusion.33 = bf16[2048,896]{0,1:T(8,128)(2,1)} fusion(bf16[2048,2304]{1,0:T(8,128)(2,1)} %convolution_convert_fusion.1, bf16[2,896,2304]{2,1,0:T(8,128)(2,1)} %param.14, f32[2048,2304]{1,0:T(8,128)} %get-tuple-element.29), kind=kOutput, calls=%fused_computation.57 | convolution fusion | flops 8484028416 | bytes 36110336 | tf_op jit(solution)/shard_map/transpose(jvp())/dot_general | solution.py:22
  148.2 18.0 %fusion.53 = bf16[1,896,2304]{2,1,0:T(8,128)(2,1)} fusion(bf16[2048,2304]{1,0:T(8,128)(2,1)} %convolution_convert_fusion.1, bf16[2048,896]{0,1:T(8,128)(2,1)} %copy-done.5, f32[2048]{0:T(1024)S(1)} %fusion.98, f32[2048,2304]{1,0:T(8,128)} %get-tuple-element.29), kind=kOutput, calls=%fused_computation.88 | convolution fusion | flops 8491597824 | bytes 36118528 | tf_op jit(solution)/shard_map/transpose(jvp())/dot_general | solution.py:22
  166.2 19.7 %fusion.55 = bf16[1,2304,896]{2,1,0:T(8,128)(2,1)} fusion(f32[2048,2304]{1,0:T(8,128)} %fusion.57, bf16[1,2048,896]{2,1,0:T(8,128)(2,1)} %param.12, f32[2048,2304]{1,0:T(8,128)} %get-tuple-element.29), kind=kOutput, calls=%fused_computation.90 | convolution fusion | flops 8486092800 | bytes 45547520 | tf_op jit(solution)/shard_map/transpose(jvp())/dot_general | solution.py:10
  185.9 14.6 %fusion.54 = bf16[1,896,2304]{2,1,0:T(8,128)(2,1)} fusion(bf16[2048,2304]{1,0:T(8,128)(2,1)} %get-tuple-element.28, bf16[2048,896]{0,1:T(8,128)(2,1)} %copy-done.5, f32[2048]{0:T(1024)S(1)} %fusion.98), kind=kOutput, calls=%fused_computation.89 | convolution fusion | flops 8461221888 | bytes 17244160 | tf_op jit(solution)/shard_map/transpose(jvp())/dot_general | solution.py:21
  200.4 0.0 slice-start.1
  200.5 14.0 %fusion.42 = (f32[2048]{0:T(1024)S(1)}, bf16[2048,896]{0,1:T(8,128)(2,1)S(1)}) fusion(bf16[2048,896]{0,1:T(8,128)(2,1)S(1)} %copy-done.6, bf16[2048,896]{0,1:T(8,128)(2,1)} %fusion.33, bf16[2048,2304]{1,0:T(8,128)(2,1)} %get-tuple-element.28, bf16[2,896,2304]{2,1,0:T(8,128)(2,1)} %param.13), kind=kOutput, calls=%fused_computation.78 | convolution fusion | flops 8464889856 | bytes 24584192 | tf_op jit(solution)/shard_map/transpose(jvp())/dot_general | solution.py:21
  214.5 4.6 fusion.76
  219.1 14.6 %convolution_convert_fusion = bf16[2048,2304]{1,0:T(8,128)(2,1)} fusion(bf16[2048,896]{0,1:T(8,128)(2,1)} %fusion.76, bf16[2,2304,896]{2,1,0:T(8,128)(2,1)S(1)} %bitcast.75), kind=kOutput, calls=%fused_computation.62 | convolution fusion | flops 8460435456 | bytes 17235968 | tf_op jit(solution)/shard_map/transpose(jvp())/dot_general | solution.py:10
  233.7 14.1 %fusion.56 = bf16[1,2304,896]{2,1,0:T(8,128)(2,1)} fusion(bf16[2048,2304]{1,0:T(8,128)(2,1)} %get-tuple-element.24, bf16[2048,896]{0,1:T(8,128)(2,1)S(1)} %copy-done.7), kind=kOutput, calls=%fused_computation.91 | convolution fusion | flops 8457781248 | bytes 17235968 | tf_op jit(solution)/shard_map/transpose(jvp())/dot_general | solution.py:10
  247.8 0.0 copy-done.11
  247.8 17.1 %fusion.49 = bf16[1,896,2304]{2,1,0:T(8,128)(2,1)} fusion(bf16[2048,2304]{1,0:T(8,128)(2,1)} %convolution_convert_fusion, bf16[1,2048,896]{1,2,0:T(8,128)(2,1)S(1)} %copy-done.2, f32[2048]{0:T(1024)S(1)} %copy-done.11, f32[2048,2304]{1,0:T(8,128)} %fusion.70), kind=kOutput, calls=%fused_computation.86 | convolution fusion | flops 8491597824 | bytes 36118528 | tf_op jit(solution)/shard_map/transpose(jvp())/dot_general | solution.py:22
  264.9 21.0 %fusion.50 = bf16[1,896,2304]{2,1,0:T(8,128)(2,1)} fusion(f32[2048,2304]{1,0:T(8,128)} %fusion.70, f32[2048,2304]{1,0:T(8,128)} %get-tuple-element.25, bf16[2048,2304]{1,0:T(8,128)(2,1)} %convolution_convert_fusion, bf16[1,2048,896]{1,2,0:T(8,128)(2,1)S(1)} %copy-done.2, f32[2048]{0:T(1024)S(1)} %copy-done.11), kind=kOutput, calls=%fused_computation.87 | convolution fusion | flops 8515190784 | bytes 54992896 | tf_op jit(solution)/shard_map/transpose(jvp())/dot_general | solution.py:21
  285.9 0.0 all-reduce.3.cloned.1.call-update
  285.9 272.6 %all-reduce.3.cloned.1.call-done = (bf16[1,896,2304]{2,1,0:T(8,128)(2,1)}, bf16[1,896,2304]{2,1,0:T(8,128)(2,1)}, bf16[1,896,2304]{2,1,0:T(8,128)(2,1)}, bf16[1,...) async-done(((bf16[1,896,2304]{2,1,0:T(8,128)(2,1)}, bf16[1,896,2304]{2,1,0:T(8,128)(2,1)}, bf16[1,896,2304]{2,1,0:T(8,128)(2,1)}, ...) | async-done | bytes 24772624 | tf_op jit(solution)/shard_map/psum | solution.py:50
  558.5 8.4 %fusion.20 = f32[]{:T(128)} fusion(bf16[1,896,2304]{2,1,0:T(8,128)(2,1)} %get-tuple-element.9, bf16[1,896,2304]{2,1,0:T(8,128)(2,1)} %get-tuple-element.10), kind=kLoop, calls=%fused_computation.44 | loop fusion | flops 16515071 | bytes 8257540 | tf_op jit(solution)/shard_map/reduce_sum | solution.py:52
  566.9 0.0 copy-done.1
  567.0 4.8 fusion.21
  573.1 8.3 %fusion.22 = f32[]{:T(128)} fusion(bf16[1,2304,896]{2,1,0:T(8,128)(2,1)} %get-tuple-element.13, bf16[1,2304,896]{2,1,0:T(8,128)(2,1)} %get-tuple-element.14), kind=kLoop, calls=%fused_computation.46 | loop fusion | flops 16515071 | bytes 8257540 | tf_op jit(solution)/shard_map/reduce_sum | solution.py:52
  582.1 28.9 %fusion.28 = (bf16[2,2304,896]{2,1,0:T(8,128)(2,1)}, f32[2,2304,896]{2,1,0:T(8,128)}, f32[2,2304,896]{2,1,0:T(8,128)}) fusion(bf16[2,2304,896]{2,1,0:T(8,128)(2,1)} %param.15, f32[]{:T(128)S(6)} %min_shard_map.3, bf16[1,2304,896]{2,1,0:T(8,128)(2,1)} %get-tuple-element.13, bf16[1,2304,896]{2,1,0:T(8,128)(2,1)} %get-tuple-element.14, ...), kind=kLoop, calls=%fused_computation.52 | loop fusion | flops 82575360 | bytes 90832896 | tf_op jit(solution)/shard_map/convert_element_type | solution.py:30
  610.9 57.8 %fusion.19 = (bf16[2,896,2304]{2,1,0:T(8,128)(2,1)}, f32[2,896,2304]{2,1,0:T(8,128)}, f32[2,896,2304]{2,1,0:T(8,128)}, bf16[2,896,2304]{2,1,0:T(8,128)(2,1)}, f3...) fusion(bf16[2,896,2304]{2,1,0:T(8,128)(2,1)} %param.13, f32[]{:T(128)S(6)} %min_shard_map.3, ...), kind=kLoop, calls=%fused_computation.43 | loop fusion | flops 165150720 | bytes 181665792 | tf_op jit(solution)/shard_map/convert_element_type | solution.py:30
  (27 shorter events, 0.1 us)
Async XLA Ops:
  7.2 551.4 %all-reduce.3.cloned.1.call-start = ((), (), s32[]{:S(2)}) async-start(), calls=%async_computation | async-start | bytes 49545216 | tf_op jit(solution)/shard_map/psum | solution.py:50
  16.1 36.9 %copy-start.10 = (f32[2048]{0:T(1024)}, f32[2048]{0:T(1024)S(1)}, u32[]{:S(2)}) copy-start(f32[2048]{0:T(1024)S(1)} %add_rsqrt_fusion) | copy-start | bytes 24580
  22.3 15.2 %copy-start.4 = (bf16[1,2048,896]{2,1,0:T(8,128)(2,1)S(1)}, bf16[1,2048,896]{2,1,0:T(8,128)(2,1)}, u32[]{:S(2)}) copy-start(bf16[1,2048,896]{2,1,0:T(8,128)(2,1)} %param.11) | copy-start | bytes 11010052
  88.7 16.4 %copy-start.5 = (bf16[2048,896]{0,1:T(8,128)(2,1)}, bf16[2048,896]{0,1:T(8,128)(2,1)S(1)}, u32[]{:S(2)}) copy-start(bf16[2048,896]{0,1:T(8,128)(2,1)S(1)} %get-tuple-element.27) | copy-start | bytes 11010052
  88.7 16.4 %copy-start.8 = (f32[2048]{0:T(1024)}, f32[2048]{0:T(1024)S(1)}, u32[]{:S(2)}) copy-start(f32[2048]{0:T(1024)S(1)} %get-tuple-element.26) | copy-start | bytes 24580
  185.9 14.6 %copy-start.6 = (bf16[2048,896]{0,1:T(8,128)(2,1)S(1)}, bf16[2048,896]{0,1:T(8,128)(2,1)}, u32[]{:S(2)}) copy-start(bf16[2048,896]{0,1:T(8,128)(2,1)} %copy-done.5) | copy-start | bytes 11010052
  185.9 33.2 %slice-start = ((s8[8257536]{0:T(1024)(128)(4,1)}), s8[4194304]{0:T(1024)(128)(4,1)S(1)}, s32[]{:S(2)}) async-start(s8[8257536]{0:T(1024)(128)(4,1)} %bitcast.74), calls=%async_computation.1 | async-start | bytes 8388608
  200.4 14.0 %copy-start.9 = (f32[2048]{0:T(1024)S(1)}, f32[2048]{0:T(1024)}, u32[]{:S(2)}) copy-start(f32[2048]{0:T(1024)} %copy-done.8) | copy-start | bytes 24580
  200.4 14.0 %copy-start.3 = (bf16[1,2048,896]{1,2,0:T(8,128)(2,1)S(1)}, bf16[1,2048,896]{1,2,0:T(8,128)(2,1)}, u32[]{:S(2)}) copy-start(bf16[1,2048,896]{1,2,0:T(8,128)(2,1)} %copy.21) | copy-start | bytes 11010052
  200.4 18.7 %slice-start.1 = ((s8[8257536]{0:T(1024)(128)(4,1)}), s8[4063232]{0:T(1024)(128)(4,1)S(1)}, s32[]{:S(2)}) async-start(s8[8257536]{0:T(1024)(128)(4,1)} %bitcast.74), calls=%async_computation.2 | async-start | bytes 8126464
  219.1 14.6 %copy-start.7 = (bf16[2048,896]{0,1:T(8,128)(2,1)S(1)}, bf16[2048,896]{0,1:T(8,128)(2,1)}, u32[]{:S(2)}) copy-start(bf16[2048,896]{0,1:T(8,128)(2,1)} %fusion.76) | copy-start | bytes 11010052
  233.7 14.1 %copy-start.2 = (bf16[1,2048,896]{1,2,0:T(8,128)(2,1)S(1)}, bf16[1,2048,896]{1,2,0:T(8,128)(2,1)}, u32[]{:S(2)}) copy-start(bf16[1,2048,896]{1,2,0:T(8,128)(2,1)} %copy.20) | copy-start | bytes 11010052
  233.7 14.1 %copy-start.11 = (f32[2048]{0:T(1024)S(1)}, f32[2048]{0:T(1024)}, u32[]{:S(2)}) copy-start(f32[2048]{0:T(1024)} %copy-done.10) | copy-start | bytes 24580
  558.5 8.4 %copy-start = (bf16[1,896,2304]{2,1,0:T(8,128)(2,1)S(1)}, bf16[1,896,2304]{2,1,0:T(8,128)(2,1)}, u32[]{:S(2)}) copy-start(bf16[1,896,2304]{2,1,0:T(8,128)(2,1)} %get-tuple-element.11) | copy-start | bytes 12386308
  558.5 8.4 %copy-start.1 = (bf16[1,896,2304]{2,1,0:T(8,128)(2,1)S(1)}, bf16[1,896,2304]{2,1,0:T(8,128)(2,1)}, u32[]{:S(2)}) copy-start(bf16[1,896,2304]{2,1,0:T(8,128)(2,1)} %get-tuple-element.12) | copy-start | bytes 12386308
Sparse Core Ops, SparseCore 0:
  286.1 272.4 all-reduce.2
where the time goes:
time: 684 us; the launch traced here: 676 us
  waiting for transfers between devices  273 us (40%)
  matrix products  259 us (38%)
  other arithmetic  116 us (17%)
  between operations  16.6 us (2%)
  local copies, waits for them, and re-layouts  12.3 us (2%)
    psum x1, waiting for transfers between devices, step(): summed[number] = [lax.psum(by_w[name], 'dp') for name in NAMES]  273 us
    dot_general x5, matrix products, layer(): gate = jnp.dot(a, w['w_gate'], preferred_element_type=jnp.float32)  91.4 us
    dot_general x5, matrix products, layer(): up = jnp.dot(a, w['w_up'], preferred_element_type=jnp.float32)  89.8 us
    convert_element_type x2, other arithmetic, adamw(): return ((w - 0.02 * step).astype(jnp.bfloat16), m, v)  86.6 us
    dot_general x5, matrix products, matmul(): jnp.dot(a, w, preferred_element_type=jnp.float32).astype(jnp.bfloat16)  77.7 us
    reduce_sum x3, other arithmetic, step(): jnp.sum(g * g)  21.5 us
  transfers between devices with their start and end apart: 1, of which 1 were waited for; matrix products, arithmetic and copies ran while one was open for 0% of the time, Pallas kernels for 0%

commit v1 on v0

v1 whole, which is shorter than its diff:
```python
import functools

import jax
import jax.numpy as jnp
from jax import lax
from jax.experimental import pallas as pl
from jax.experimental.pallas import tpu as pltpu
from jax.sharding import PartitionSpec as P

T, D, F = 2048, 896, 2304
FB = 256
NB = F // FB
LAYERS = 2
NBLK = NB * LAYERS
COUNT = 3 * LAYERS * D * F
TM = 256
f32, bf16 = jnp.float32, jnp.bfloat16
MESH = pl.DeviceIdType.MESH
VMEM_LIMIT = 63 * 2**20
ANY = pl.BlockSpec(memory_space=pl.ANY)
VMEM = pl.BlockSpec(memory_space=pltpu.VMEM)
sds = jax.ShapeDtypeStruct


def dot(a, b):
    return jnp.dot(a, b, preferred_element_type=f32)


def dot_t(a, b):
    return lax.dot_general(a, b, (((1,), (1,)), ((), ())), preferred_element_type=f32)


def norm_scale(h):
    return lax.rsqrt(jnp.mean(h * h, -1, keepdims=True) + 1e-6)


def rows(t):
    return pl.ds(pl.multiple_of(t * TM, TM), TM)


def block(b):
    return pl.ds(pl.multiple_of(b * FB, FB), FB)


def forward(x_ref, wg, wu, wd_hbm, s_hbm, a_hbm, act_hbm, h1_ref, a0t_ref, a0, act, wgb, wub, wd, sb, ab, wsem, wdsem, osem):
    def fetch(b, slot):
        return (
            pltpu.make_async_copy(wg.at[0, :, block(b)], wgb.at[slot], wsem.at[slot, 0]),
            pltpu.make_async_copy(wu.at[0, :, block(b)], wub.at[slot], wsem.at[slot, 1]),
        )

    for c in fetch(0, 0):
        c.start()
    whole = pltpu.make_async_copy(wd_hbm.at[0], wd, wdsem)
    whole.start()

    @pl.loop(0, T // TM)
    def _(t):
        h = x_ref[rows(t), :].astype(f32)
        a0[rows(t), :] = (h * norm_scale(h)).astype(bf16)

    @pl.loop(0, T // TM)
    def _(t):
        a0t_ref[:, rows(t)] = a0[rows(t), :].T

    def outs(b, slot):
        return (
            pltpu.make_async_copy(sb.at[slot], s_hbm.at[b], osem.at[slot, 0]),
            pltpu.make_async_copy(ab.at[slot], a_hbm.at[b], osem.at[slot, 1]),
        )

    @pl.loop(0, NB)
    def _(b):
        slot = lax.rem(b, 2)

        @pl.when(b + 1 < NB)
        def _():
            for c in fetch(b + 1, 1 - slot):
                c.start()

        for c in fetch(b, slot):
            c.wait()

        @pl.when(b >= 2)
        def _():
            for c in outs(b - 2, slot):
                c.wait()

        for t in range(T // TM):
            r = pl.ds(t * TM, TM)
            gate = dot(a0[r, :], wgb[slot])
            up = dot(a0[r, :], wub[slot])
            sg = 1.0 / (1.0 + jnp.exp(-gate))
            s = gate * sg
            act[b, r, :] = (s * up).astype(bf16)
            sb[slot, r, :] = s
            ab[slot, r, :] = up * (sg + s * (1.0 - sg))
        for c in outs(b, slot):
            c.start()

    keep = pltpu.make_async_copy(act, act_hbm, wdsem)
    whole.wait()
    keep.start()

    @pl.loop(0, T // TM)
    def _(t):
        total = dot(act[0, rows(t), :], wd[0:FB, :])
        for b in range(1, NB):
            total += dot(act[b, rows(t), :], wd[b * FB : (b + 1) * FB, :])
        h1_ref[rows(t), :] = x_ref[rows(t), :] + total.astype(bf16)

    for b in (NB - 2, NB - 1):
        for c in outs(b, b % 2):
            c.wait()
    keep.wait()


def run_forward(x, wg, wu, wd):
    return pl.pallas_call(
        forward,
        name="forward",
        out_shape=(sds((NB, T, FB), f32), sds((NB, T, FB), f32), sds((NB, T, FB), bf16), sds((T, D), bf16), sds((D, T), bf16)),
        in_specs=[VMEM, ANY, ANY, ANY],
        out_specs=(ANY, ANY, ANY, VMEM, VMEM),
        scratch_shapes=[
            pltpu.VMEM((T, D), bf16),
            pltpu.VMEM((NB, T, FB), bf16),
            pltpu.VMEM((2, D, FB), bf16),
            pltpu.VMEM((2, D, FB), bf16),
            pltpu.VMEM((F, D), bf16),
            pltpu.VMEM((2, T, FB), f32),
            pltpu.VMEM((2, T, FB), f32),
            pltpu.SemaphoreType.DMA((2, 2)),
            pltpu.SemaphoreType.DMA,
            pltpu.SemaphoreType.DMA((2, 2)),
        ],
        compiler_params=pltpu.CompilerParams(vmem_limit_bytes=VMEM_LIMIT),
    )(x, wg, wu, wd)


STRIDE = (16, 4, 1)
START = (0, 3, 7, 10)
NS, NG, NL = 3, 3, 6
LAST = 14


def comm_scratch():
    def v(*shape):
        return pltpu.VMEM((*shape, 16, 128), bf16)

    return dict(
        blk=v(NS, 3, 56, 2),
        r1=v(2, 3, 2, 7, 2),
        c2=v(3, 2, 28),
        r2=v(2, 3, 2, 28),
        q1=v(2, 3, 28),
        r3a=v(2, 3, 4),
        r3b=v(2, 3, 3),
        c4=v(3, 2, 7),
        r4=v(2, 3, 2, 7),
        q2=v(2, 3, 4, 2),
        r5=v(2, 3, 2, 1),
        c6=v(3, 2, 2),
        r6=v(2, 3, 2, 2),
        g3=v(NG, 3, 4, 2),
        whole=v(NL, 3, 112),
        ssq=pltpu.VMEM((8, 128), f32),
        ssq_to=pltpu.VMEM((6, 8, 128), f32),
        ssq_from=pltpu.VMEM((6, 8, 128), f32),
        send=pltpu.SemaphoreType.DMA((12, 3, 2)),
        recv=pltpu.SemaphoreType.DMA((12, 2, 3, 2)),
        osem=pltpu.SemaphoreType.DMA((2,)),
        qsend=pltpu.SemaphoreType.DMA((6,)),
        qrecv=pltpu.SemaphoreType.DMA((6,)),
    )


def at(p, k):
    return lax.rem(p + k, 4)


def add(*terms):
    total = terms[0].astype(f32)
    for t in terms[1:]:
        total = total + t.astype(f32)
    return total


class Comm:
    def __init__(self, refs, g_hbm):
        self.__dict__.update(refs)
        self.g_hbm = g_hbm
        me = lax.axis_index("dp")
        self.pos = [lax.rem(lax.div(me, s), 4) for s in STRIDE]
        self.near = [(me - p * s + at(p, 1) * s, me - p * s + at(p, 3) * s) for p, s in zip(self.pos, STRIDE)]
        self.ssq[...] = jnp.zeros((8, 128), f32)

    def barrier(self):
        sem = pltpu.get_barrier_semaphore()
        for pair in self.near:
            for device in pair:
                pl.semaphore_signal(sem, inc=1, device_id={"dp": device}, device_id_type=MESH)
        pl.semaphore_wait(sem, 6)

    def place(self, j):
        d = tuple((j + k) % 3 for k in range(3))
        return d, tuple(self.pos[k] for k in d)

    def copies(self, stage, b):
        s, bs, gs, ws = lax.rem(b, 2), lax.rem(b, NS), lax.rem(b, NG), lax.rem(b, NL)
        out = []

        def put(j, way, d, src, dst):
            out.append(
                pltpu.make_async_remote_copy(
                    src_ref=src,
                    dst_ref=dst,
                    send_sem=self.send.at[stage - 1, j, way],
                    recv_sem=self.recv.at[stage - 1, s, j, way],
                    device_id={"dp": self.near[d][way]},
                    device_id_type=MESH,
                )
            )

        for j in range(3):
            (d0, d1, d2), (p0, p1, p2) = self.place(j)
            for w in range(2):
                back = 3 - 2 * w
                if stage == 1:
                    put(j, w, d0, self.blk.at[bs, j, pl.ds(at(p0, 2) * 14 + 7 * w, 7)], self.r1.at[s, j, w])
                elif stage == 2:
                    put(j, w, d0, self.c2.at[j, w], self.r2.at[s, j, w])
                elif stage == 3:
                    put(j, w, d1, self.q1.at[s, j, pl.ds(at(p1, 2) * 7 + 4 * w, 4 - w)], (self.r3b if w else self.r3a).at[s, j])
                elif stage == 4:
                    put(j, w, d1, self.c4.at[j, w], self.r4.at[s, j, w])
                elif stage == 5:
                    put(j, w, d2, self.q2.at[s, j, at(p2, 2), pl.ds(w, 1)], self.r5.at[s, j, w])
                elif stage == 6:
                    put(j, w, d2, self.c6.at[j, w], self.r6.at[s, j, w])
                elif stage == 7:
                    put(j, w, d2, self.g3.at[gs, j, p2], self.g3.at[gs, j, p2])
                elif stage == 8:
                    part = self.g3.at[gs, j, at(p2, back), pl.ds(w, 1)]
                    put(j, w, d2, part, part)
                else:
                    if stage == 9:
                        start, n = p0 * 28 + p1 * 7, 7
                    elif stage == 10:
                        start, n = p0 * 28 + at(p1, back) * 7 + 4 * w, 4 - w
                    elif stage == 11:
                        start, n = p0 * 28, 28
                    else:
                        start, n = at(p0, back) * 28 + 14 * w, 14
                    part = self.whole.at[ws, j, pl.ds(start, n)]
                    put(j, w, d0 if stage > 10 else d1, part, part)
        return out

    def math(self, stage, b):
        s, bs, gs, ws = lax.rem(b, 2), lax.rem(b, NS), lax.rem(b, NG), lax.rem(b, NL)
        for j in range(3):
            _, (p0, p1, p2) = self.place(j)
            if stage == 2:

                def own(k, half):
                    return self.blk[bs, j, pl.ds(at(p0, k) * 14 + 7 * half, 7)].reshape(14, 16, 128)

                def came(w):
                    return self.r1[s, j, w].reshape(14, 16, 128)

                self.c2[j, 0, 0:14] = add(own(1, 0), came(0)).astype(bf16)
                self.c2[j, 0, 14:28] = own(1, 1)
                self.c2[j, 1, 0:14] = own(3, 0)
                self.c2[j, 1, 14:28] = add(own(3, 1), came(1)).astype(bf16)
            elif stage == 3:
                mine = self.blk[bs, j, pl.ds(p0 * 14, 14)].reshape(28, 16, 128)
                self.q1[s, j] = add(mine, self.r2[s, j, 0], self.r2[s, j, 1]).astype(bf16)
            elif stage == 4:

                def own(k, start, n):
                    return self.q1[s, j, pl.ds(at(p1, k) * 7 + start, n)]

                self.c4[j, 0, 0:4] = add(own(1, 0, 4), self.r3a[s, j]).astype(bf16)
                self.c4[j, 0, 4:7] = own(1, 4, 3)
                self.c4[j, 1, 0:4] = own(3, 0, 4)
                self.c4[j, 1, 4:7] = add(own(3, 4, 3), self.r3b[s, j]).astype(bf16)
            elif stage == 5:
                total = add(self.q1[s, j, pl.ds(p1 * 7, 7)], self.r4[s, j, 0], self.r4[s, j, 1]).reshape(14, 8, 128)
                for k, start in enumerate(START):
                    self.q2[s, j, k] = total[start : start + 4].reshape(2, 16, 128).astype(bf16)
            elif stage == 6:

                def own(k, half):
                    return self.q2[s, j, at(p2, k), pl.ds(half, 1)]

                self.c6[j, 0, 0:1] = add(own(1, 0), self.r5[s, j, 0]).astype(bf16)
                self.c6[j, 0, 1:2] = own(1, 1)
                self.c6[j, 1, 0:1] = own(3, 0)
                self.c6[j, 1, 1:2] = add(own(3, 1), self.r5[s, j, 1]).astype(bf16)
            elif stage == 7:
                g = add(self.q2[s, j, p2], self.r6[s, j, 0], self.r6[s, j, 1]).astype(bf16)
                self.g3[gs, j, p2] = g
                square = g.astype(f32).reshape(4, 8, 128)
                square = square * square
                self.ssq[...] += square[0] * jnp.where(lax.rem(p2, 2) == 1, 0.0, 1.0) + square[1] + square[2] + square[3]
            elif stage == 9:
                g = self.g3[gs, j].astype(f32).reshape(4, 4, 8, 128)
                g = jnp.concatenate([g[0], g[1, 1:], g[2], g[3, 1:]], axis=0)
                self.whole[ws, j, pl.ds(p0 * 28 + p1 * 7, 7)] = g.reshape(7, 16, 128).astype(bf16)

    def out(self, b):
        return pltpu.make_async_copy(self.whole.at[lax.rem(b, NL)], self.g_hbm.at[b], self.osem.at[lax.rem(b, 2)])

    def stage(self, k, b):
        if 2 <= k <= 13:
            for c in self.copies(k - 1, b):
                c.wait()
        if k <= 12:
            self.math(k, b)
            for c in self.copies(k, b):
                c.start()
        elif k == 13:
            self.out(b).start()
        else:
            self.out(b).wait()

    def service(self, i):
        for k in range(LAST, 0, -1):
            pl.when((i >= k) & (i - k < NBLK))(functools.partial(self.stage, k, i - k))

    def total(self):
        for step in range(6):
            d, odd = divmod(step, 2)
            forth = lax.rem(self.pos[d], 2) == odd
            self.ssq_to[step] = self.ssq[...]
            c = pltpu.make_async_remote_copy(
                src_ref=self.ssq_to.at[step],
                dst_ref=self.ssq_from.at[step],
                send_sem=self.qsend.at[step],
                recv_sem=self.qrecv.at[step],
                device_id={"dp": jnp.where(forth, *self.near[d])},
                device_id_type=MESH,
            )
            c.start()
            c.wait()
            self.ssq[...] += self.ssq_from[step]


def backward(names, h1_hbm, dy_hbm, a0t_hbm, s_hbm, a_hbm, act_hbm, wg, wu, wd, g_hbm, ssq_out, *scratch):
    refs = dict(zip(names, scratch, strict=True))
    h1, dy, a, a_t, dy_t, da, wgb, wub, wdb, act, dg, du, sb, ab, isem, wsem = (refs.pop(n) for n in OWN)
    comm = Comm(refs, g_hbm)
    first = [pltpu.make_async_copy(src, dst, isem.at[k]) for k, (src, dst) in enumerate(((h1_hbm, h1), (dy_hbm, dy)))]
    for c in first:
        c.start()

    def fetch1(b, slot):
        return (
            pltpu.make_async_copy(wg.at[1, :, block(b)], wgb.at[slot], wsem.at[slot, 0]),
            pltpu.make_async_copy(wu.at[1, :, block(b)], wub.at[slot], wsem.at[slot, 1]),
            pltpu.make_async_copy(wd.at[1, block(b), :], wdb.at[slot], wsem.at[slot, 2]),
        )

    def fetch0(b, slot):
        return (
            pltpu.make_async_copy(s_hbm.at[b], sb.at[slot], wsem.at[slot, 0]),
            pltpu.make_async_copy(a_hbm.at[b], ab.at[slot], wsem.at[slot, 1]),
            pltpu.make_async_copy(act_hbm.at[b], act.at[slot], wsem.at[slot, 3]),
            pltpu.make_async_copy(wd.at[0, block(b), :], wdb.at[slot], wsem.at[slot, 2]),
        )

    for c in fetch1(0, 0):
        c.start()
    comm.barrier()
    for c in first:
        c.wait()

    @pl.loop(0, T // TM)
    def _(t):
        h = h1[rows(t), :].astype(f32)
        a[rows(t), :] = (h * norm_scale(h)).astype(bf16)

    @pl.loop(0, T // TM)
    def _(t):
        a_t[:, rows(t)] = a[rows(t), :].T
        dy_t[:, rows(t)] = dy[rows(t), :].T
        da[rows(t), :] = jnp.zeros((TM, D), f32)

    def give(slot, j, g):
        for half in range(2):
            comm.blk[slot, j, :, half] = g[:, half * 128 : (half + 1) * 128].astype(bf16).reshape(56, 16, 128)

    @pl.loop(0, NB)
    def _(b):
        comm.service(b)
        slot, to = lax.rem(b, 2), lax.rem(b, NS)

        @pl.when(b + 1 < NB)
        def _():
            for c in fetch1(b + 1, 1 - slot):
                c.start()

        for c in fetch1(b, slot):
            c.wait()
        for t in range(T // TM):
            r = pl.ds(t * TM, TM)
            gate = dot(a[r, :], wgb[slot])
            up = dot(a[r, :], wub[slot])
            dact = dot_t(dy[r, :], wdb[slot]).astype(bf16).astype(f32)
            sg = 1.0 / (1.0 + jnp.exp(-gate))
            s = gate * sg
            act[0, r, :] = (s * up).astype(bf16)
            dgate = (dact * up * (sg + s * (1.0 - sg))).astype(bf16)
            dup = (dact * s).astype(bf16)
            dg[r, :] = dgate
            du[r, :] = dup
            da[r, :] += dot_t(dgate, wgb[slot]) + dot_t(dup, wub[slot])
        give(to, 0, dot(a_t[...], dg[...]))
        give(to, 1, dot(a_t[...], du[...]))
        give(to, 2, dot(dy_t[...], act[0]))

    for c in fetch0(0, 0):
        c.start()
    last = pltpu.make_async_copy(a0t_hbm, a_t, isem.at[0])
    last.start()

    @pl.loop(0, T // TM)
    def _(t):
        h = h1[rows(t), :].astype(f32)
        scale = norm_scale(h)
        g = da[rows(t), :].astype(bf16).astype(f32)
        along = jnp.mean(g * h, -1, keepdims=True)
        dh = (g * scale - h * (scale * scale * scale * along)).astype(bf16) + dy[rows(t), :]
        dy[rows(t), :] = dh
        dy_t[:, rows(t)] = dh.T

    last.wait()

    @pl.loop(0, NB)
    def _(b):
        comm.service(b + NB)
        slot, to = lax.rem(b, 2), lax.rem(b + NB, NS)

        @pl.when(b + 1 < NB)
        def _():
            for c in fetch0(b + 1, 1 - slot):
                c.start()

        for c in fetch0(b, slot):
            c.wait()
        for t in range(T // TM):
            r = pl.ds(t * TM, TM)
            dact = dot_t(dy[r, :], wdb[slot]).astype(bf16).astype(f32)
            dg[r, :] = (dact * ab[slot, r, :]).astype(bf16)
            du[r, :] = (dact * sb[slot, r, :]).astype(bf16)
        give(to, 0, dot(a_t[...], dg[...]))
        give(to, 1, dot(a_t[...], du[...]))
        give(to, 2, dot(dy_t[...], act[slot]))

    @pl.loop(NBLK, NBLK + LAST)
    def _(i):
        comm.service(i)

    comm.total()
    ssq_out[...] = comm.ssq[...]


OWN = ("h1", "dy", "a", "a_t", "dy_t", "da", "wgb", "wub", "wdb", "act", "dg", "du", "sb", "ab", "isem", "wsem")


def run_backward(h1, dy, a0t, s, a, act, wg, wu, wd):
    own = dict(
        h1=pltpu.VMEM((T, D), bf16),
        dy=pltpu.VMEM((T, D), bf16),
        a=pltpu.VMEM((T, D), bf16),
        a_t=pltpu.VMEM((D, T), bf16),
        dy_t=pltpu.VMEM((D, T), bf16),
        da=pltpu.VMEM((T, D), f32),
        wgb=pltpu.VMEM((2, D, FB), bf16),
        wub=pltpu.VMEM((2, D, FB), bf16),
        wdb=pltpu.VMEM((2, FB, D), bf16),
        act=pltpu.VMEM((2, T, FB), bf16),
        dg=pltpu.VMEM((T, FB), bf16),
        du=pltpu.VMEM((T, FB), bf16),
        sb=pltpu.VMEM((2, T, FB), f32),
        ab=pltpu.VMEM((2, T, FB), f32),
        isem=pltpu.SemaphoreType.DMA((2,)),
        wsem=pltpu.SemaphoreType.DMA((2, 4)),
    )
    scratch = own | comm_scratch()
    return pl.pallas_call(
        functools.partial(backward, tuple(scratch)),
        name="backward",
        out_shape=(sds((NBLK, 3, 112, 16, 128), bf16), sds((8, 128), f32)),
        in_specs=[ANY] * 9,
        out_specs=(ANY, VMEM),
        scratch_shapes=list(scratch.values()),
        compiler_params=pltpu.CompilerParams(collective_id=0, has_side_effects=True, vmem_limit_bytes=VMEM_LIMIT),
    )(h1, dy, a0t, s, a, act, wg, wu, wd)


def adamw(ssq_ref, g_ref, *refs):
    factor = jnp.minimum(1.0, 0.5 * lax.rsqrt(jnp.sum(ssq_ref[...], keepdims=True) / COUNT + 1e-30))
    ins, outs = refs[:9], refs[9:]

    def update(k, where, g):
        w, m, v = (ins[i + k][where].astype(f32) for i in (0, 3, 6))
        g = g.astype(f32) * factor
        m = 0.9 * m + 0.1 * g
        v = 0.95 * v + 0.05 * g * g
        step = m * lax.rsqrt(v + 1e-8) + 0.1 * w
        outs[k][where] = (w - 0.02 * step).astype(bf16)
        outs[3 + k][where] = m
        outs[6 + k][where] = v

    @pl.loop(0, 7)
    def _(n):
        tiles = pl.ds(n * 16, 16)
        at_rows = pl.ds(pl.multiple_of(n * 128, 128), 128)
        for k in range(3):
            g = g_ref[0, k, tiles].reshape(8, 2, 16, 128)
            for half in range(2):
                cols = pl.ds(half * 128, 128)
                part = g[:, half].reshape(128, 128)
                if k < 2:
                    update(k, (0, at_rows, cols), part)
                else:
                    update(k, (0, cols, at_rows), part.astype(f32).T)


def run_adamw(ssq, g, *arrays):
    def of(i):
        return 1 - i // NB, i % NB

    wide = pl.BlockSpec((1, D, FB), lambda i: (of(i)[0], 0, of(i)[1]))
    tall = pl.BlockSpec((1, FB, D), lambda i: (of(i)[0], of(i)[1], 0))
    specs = [wide, wide, tall] * 3
    return pl.pallas_call(
        adamw,
        name="adamw",
        grid=(NBLK,),
        out_shape=tuple(sds(a.shape, a.dtype) for a in arrays),
        in_specs=[pl.BlockSpec((8, 128), lambda i: (0, 0)), pl.BlockSpec((1, 3, 112, 16, 128), lambda i: (i, 0, 0, 0, 0))] + specs,
        out_specs=tuple(specs),
        compiler_params=pltpu.CompilerParams(vmem_limit_bytes=VMEM_LIMIT, dimension_semantics=("arbitrary",)),
    )(ssq, g, *arrays)


def solution(mesh):
    def step(x, dy, *arrays):
        wg, wu, wd = arrays[:3]
        s, a, act, h1, a0t = run_forward(x[0], wg, wu, wd)
        g, ssq = run_backward(h1, dy[0], a0t, s, a, act, wg, wu, wd)
        return run_adamw(ssq, g, *arrays)

    return jax.shard_map(
        step,
        mesh=mesh,
        in_specs=(P(("rep", "dp"), None, None),) * 2 + (P(None, None, None),) * 9,
        out_specs=(P("rep", None, None),) * 9,
        check_vma=False,
    )
```

time: 684 us -> 423 us (0.62); the launches traced: 676 us -> 423 us
  Pallas kernels: 0 us -> 422 us
  waiting for transfers between devices: 273 us -> 0 us
  matrix products: 259 us -> 0 us
  other arithmetic: 116 us -> 0 us
  between operations: 16.6 us -> 0.83 us
  local copies, waits for them, and re-layouts: 12.3 us -> 0 us
    pallas_call x0 -> x3, Pallas kernels: none -> 422 us  [the longest x1 285 us: run_backward(): pl.pallas_call(functools.partial(backward, tuple(scratch)), name='backwar...]
    psum x1 -> x0, waiting for transfers between devices: 273 us -> none  [step(): summed[number] = [lax.psum(by_w[name], 'dp') for name in NAMES]]
    dot_general x15 -> x0, matrix products: 259 us -> none  [the longest x5 91.4 us: layer(): gate = jnp.dot(a, w['w_gate'], preferred_element_type=jnp.float32)]
    convert_element_type x2 -> x0, other arithmetic: 86.6 us -> none  [adamw(): return ((w - 0.02 * step).astype(jnp.bfloat16), m, v)]
    reduce_sum x4 -> x0, other arithmetic: 24.3 us -> none  [the longest x3 21.5 us: step(): jnp.sum(g * g)]
    unnamed x30 -> x0, local copies, waits for them, and re-layouts: 12.3 us -> none
  transfers between devices with their start and end apart: 1 -> 0, of which waited for: 1 -> 0; matrix products, arithmetic and copies ran while one was open for 0% -> 0% of each run, Pallas kernels for 0% -> 0%
where the time goes in v1:
time: 423 us
  Pallas kernels  422 us (100%)
    pallas_call x1, Pallas kernels, run_backward(): pl.pallas_call(functools.partial(backward, tuple(scratch)), name='backwar...  285 us
    pallas_call x1, Pallas kernels, run_adamw(): pl.pallas_call(adamw, name='adamw', grid=(NBLK,), out_shape=tuple((sds(a....  96.6 us
    pallas_call x1, Pallas kernels, run_forward(): pl.pallas_call(forward, name='forward', out_shape=(sds((NB, T, FB), f32),...  41.1 us

profile of v1, /device:TPU:0, one launch (start us, length us, event | category | flops | bytes accessed | tf_op | source)
XLA Modules:
  0.0 423.2 jit_solution(6781225279178350908)
XLA Ops:
  0.6 41.1 %forward.1 = (f32[9,2048,256]{2,1,0:T(8,128)}, f32[9,2048,256]{2,1,0:T(8,128)}, bf16[9,2048,256]{2,1,0:T(8,128)(2,1)}, bf16[2048,896]{1,0:T(8,128)(2,1)}, bf16[896,2048]{1,0:T(8,128)(2,1)}) custom-call(bf16[2048,896]{1,0:T(8,128)(2,1)} %bitcast.2, bf16[2,896,2304]{2,1,0:T(8,128)(2,1)} %refs_0_.1, bf16[2,896,2304]{2,1,0:T(8,128)(2,1)} %refs_1_.1, ...), custom_call_target="tpu_custom_call" | custom-call | tf_op jit(solution)/shard_map/forward/pallas_call | solution.py:119
  41.8 284.6 %backward.1 = (bf16[18,3,112,16,128]{4,3,2,1,0:T(8,128)(2,1)}, f32[8,128]{1,0:T(8,128)}) custom-call(bf16[2048,896]{1,0:T(8,128)(2,1)} %get-tuple-element.16.h1_hbm, bf16[2048,896]{1,0:T(8,128)(2,1)} %bitcast.3, bf16[896,2048]{1,0:T(8,128)(2,1)} %get-tuple-element.17.a0t_hbm, f32[9,2048,256]{2,1,0:T(8,128)} %get-tuple-element.18.s_hbm, ...), custom_call_target="tpu_custom_call" | custom-call | tf_op jit(solution)/shard_map/backward/pallas_call | solution.py:491
  326.4 96.6 %adamw.1 = (bf16[2,896,2304]{2,1,0:T(8,128)(2,1)}, bf16[2,896,2304]{2,1,0:T(8,128)(2,1)}, bf16[2,2304,896]{2,1,0:T(8,128)(2,1)}, f32[2,896,2304]{2,1,0:T(8,128)}...) custom-call(f32[8,128]{1,0:T(8,128)} %get-tuple-element.21.ssq_ref, ...), custom_call_target="tpu_custom_call" | custom-call | tf_op jit(solution)/shard_map/adamw/pallas_call | solution.py:538

commit v2 on v1

v2 whole, which is shorter than its diff:
```python
import functools

import jax
import jax.numpy as jnp
from jax import lax
from jax.experimental import pallas as pl
from jax.experimental.pallas import tpu as pltpu
from jax.sharding import PartitionSpec as P

T, D, F = 2048, 896, 2304
FB = 256
NB = F // FB
LAYERS = 2
NBLK = NB * LAYERS
COUNT = 3 * LAYERS * D * F
TM = 256
f32, bf16 = jnp.float32, jnp.bfloat16
MESH = pl.DeviceIdType.MESH
VMEM_LIMIT = 63 * 2**20
ANY = pl.BlockSpec(memory_space=pl.ANY)
VMEM = pl.BlockSpec(memory_space=pltpu.VMEM)
sds = jax.ShapeDtypeStruct


def dot(a, b):
    return jnp.dot(a, b, preferred_element_type=f32)


def dot_t(a, b):
    return lax.dot_general(a, b, (((1,), (1,)), ((), ())), preferred_element_type=f32)


def norm_scale(h):
    return lax.rsqrt(jnp.mean(h * h, -1, keepdims=True) + 1e-6)


def rows(t):
    return pl.ds(pl.multiple_of(t * TM, TM), TM)


def block(b):
    return pl.ds(pl.multiple_of(b * FB, FB), FB)


def forward(x_ref, dy_ref, wg, wu, wd_hbm, s_hbm, a_hbm, act_hbm, h1_hbm, a0t_hbm, a1_hbm, a1t_hbm, dyt_hbm, a0, act, wgu, wd, sb, ab, h1, a0t, a1, a1t, dyt, wsem, wdsem, osem, tsem):
    def fetch(b, slot):
        return (
            pltpu.make_async_copy(wg.at[0, :, block(b)], wgu.at[slot, :, 0:FB], wsem.at[slot, 0]),
            pltpu.make_async_copy(wu.at[0, :, block(b)], wgu.at[slot, :, FB : 2 * FB], wsem.at[slot, 1]),
        )

    for c in fetch(0, 0):
        c.start()
    whole = pltpu.make_async_copy(wd_hbm.at[0], wd, wdsem)
    whole.start()

    @pl.loop(0, T // TM)
    def _(t):
        h = x_ref[rows(t), :].astype(f32)
        a0[rows(t), :] = (h * norm_scale(h)).astype(bf16)

    def outs(b, slot):
        return (
            pltpu.make_async_copy(sb.at[slot], s_hbm.at[b], osem.at[slot, 0]),
            pltpu.make_async_copy(ab.at[slot], a_hbm.at[b], osem.at[slot, 1]),
        )

    @pl.loop(0, NB)
    def _(b):
        slot = lax.rem(b, 2)

        @pl.when(b + 1 < NB)
        def _():
            for c in fetch(b + 1, 1 - slot):
                c.start()

        for c in fetch(b, slot):
            c.wait()

        @pl.when(b >= 2)
        def _():
            for c in outs(b - 2, slot):
                c.wait()

        turn = rows(jnp.minimum(b, T // TM - 1))
        a0t[:, turn] = a0[turn, :].T
        dyt[:, turn] = dy_ref[turn, :].T
        for t in range(T // TM):
            r = pl.ds(t * TM, TM)
            both = dot(a0[r, :], wgu[slot])
            gate, up = both[:, :FB], both[:, FB:]
            sg = 1.0 / (1.0 + jnp.exp(-gate))
            s = gate * sg
            act[r, block(b)] = (s * up).astype(bf16)
            sb[slot, r, :] = s
            ab[slot, r, :] = up * (sg + s * (1.0 - sg))
        for c in outs(b, slot):
            c.start()

    keep = [pltpu.make_async_copy(src, dst, tsem.at[k]) for k, (src, dst) in enumerate(((act, act_hbm), (a0t, a0t_hbm), (dyt, dyt_hbm)))]
    for c in keep:
        c.start()
    whole.wait()

    def tail(t):
        return (
            pltpu.make_async_copy(h1.at[rows(t), :], h1_hbm.at[rows(t), :], tsem.at[3]),
            pltpu.make_async_copy(a1.at[rows(t), :], a1_hbm.at[rows(t), :], tsem.at[4]),
            pltpu.make_async_copy(a1t.at[:, rows(t)], a1t_hbm.at[:, rows(t)], tsem.at[5]),
        )

    @pl.loop(0, T // TM)
    def _(t):
        h = x_ref[rows(t), :] + dot(act[rows(t), :], wd[...]).astype(bf16)
        h1[rows(t), :] = h
        h = h.astype(f32)
        n = (h * norm_scale(h)).astype(bf16)
        a1[rows(t), :] = n
        a1t[:, rows(t)] = n.T

        @pl.when(t > 0)
        def _():
            for c in tail(t - 1):
                c.wait()

        for c in tail(t):
            c.start()

    for c in tail(T // TM - 1):
        c.wait()
    for b in (NB - 2, NB - 1):
        for c in outs(b, b % 2):
            c.wait()
    for c in keep:
        c.wait()


def run_forward(x, dy, wg, wu, wd):
    wide, tall = (T, D), (D, T)
    return pl.pallas_call(
        forward,
        name="forward",
        out_shape=(sds((NB, T, FB), f32), sds((NB, T, FB), f32), sds((T, F), bf16), *(sds(s, bf16) for s in (wide, tall, wide, tall, tall))),
        in_specs=[VMEM, VMEM, ANY, ANY, ANY],
        out_specs=(ANY,) * 8,
        scratch_shapes=[
            pltpu.VMEM(wide, bf16),
            pltpu.VMEM((T, F), bf16),
            pltpu.VMEM((2, D, 2 * FB), bf16),
            pltpu.VMEM((F, D), bf16),
            pltpu.VMEM((2, T, FB), f32),
            pltpu.VMEM((2, T, FB), f32),
            *(pltpu.VMEM(s, bf16) for s in (wide, tall, wide, tall, tall)),
            pltpu.SemaphoreType.DMA((2, 2)),
            pltpu.SemaphoreType.DMA,
            pltpu.SemaphoreType.DMA((2, 2)),
            pltpu.SemaphoreType.DMA((6,)),
        ],
        compiler_params=pltpu.CompilerParams(vmem_limit_bytes=VMEM_LIMIT),
    )(x, dy, wg, wu, wd)


STRIDE = (16, 4, 1)
START = (0, 3, 7, 10)
NS, NG, NL = 3, 3, 6
SUMMED, LAST = 6, 12


def ready(b):
    return 2 * b + 1 if b < NB else NB + b


END = ready(NBLK - 1)


def comm_scratch():
    def v(*shape):
        return pltpu.VMEM((*shape, 16, 128), bf16)

    return dict(
        blk=v(NS, 3, 56, 2),
        r1=v(2, 3, 2, 7, 2),
        c2=v(3, 2, 28),
        r2=v(2, 3, 2, 28),
        q1=v(2, 3, 28),
        r3a=v(2, 3, 4),
        r3b=v(2, 3, 3),
        c4=v(3, 2, 7),
        r4=v(2, 3, 2, 7),
        q2=v(2, 3, 4, 2),
        r5=v(2, 3, 3, 2),
        g3=v(NG, 3, 4, 2),
        whole=v(NL, 3, 112),
        ssq=pltpu.VMEM((8, 128), f32),
        ssq_to=pltpu.VMEM((6, 8, 128), f32),
        ssq_from=pltpu.VMEM((6, 8, 128), f32),
        send=pltpu.SemaphoreType.DMA((10, 3, 2)),
        recv=pltpu.SemaphoreType.DMA((10, 2, 3, 2)),
        send3=pltpu.SemaphoreType.DMA((2, 2, 3, 3)),
        recv3=pltpu.SemaphoreType.DMA((2, 3, 3, 3)),
        osem=pltpu.SemaphoreType.DMA((2,)),
        qsend=pltpu.SemaphoreType.DMA((6,)),
        qrecv=pltpu.SemaphoreType.DMA((6,)),
    )


def at(p, k):
    return lax.rem(p + k, 4)


def add(*terms):
    total = terms[0].astype(f32)
    for t in terms[1:]:
        total = total + t.astype(f32)
    return total


class Comm:
    def __init__(self, refs, g_hbm):
        self.__dict__.update(refs)
        self.g_hbm = g_hbm
        me = lax.axis_index("dp")
        self.pos = [lax.rem(lax.div(me, s), 4) for s in STRIDE]
        self.near = [tuple(me - p * s + at(p, k) * s for k in (1, 3, 2)) for p, s in zip(self.pos, STRIDE)]
        self.ssq[...] = jnp.zeros((8, 128), f32)

    def barrier(self):
        sem = pltpu.get_barrier_semaphore()
        for ring in self.near:
            for device in ring:
                pl.semaphore_signal(sem, inc=1, device_id={"dp": device}, device_id_type=MESH)
        pl.semaphore_wait(sem, 9)

    def place(self, j):
        d = tuple((j + k) % 3 for k in range(3))
        return d, tuple(self.pos[k] for k in d)

    def copies(self, stage, b):
        s, bs, gs, ws = lax.rem(b, 2), lax.rem(b, NS), lax.rem(b, NG), lax.rem(b, NL)
        out = []

        def put(j, way, d, src, dst):
            if stage in (5, 6):
                send, recv = self.send3.at[stage - 5, s, j, way], self.recv3.at[stage - 5, lax.rem(b, 3), j, way]
            else:
                send, recv = self.send.at[stage - 1, j, way], self.recv.at[stage - 1, s, j, way]
            device = {"dp": self.near[d][way]}
            out.append(pltpu.make_async_remote_copy(src_ref=src, dst_ref=dst, send_sem=send, recv_sem=recv, device_id=device, device_id_type=MESH))

        for j in range(3):
            (d0, d1, d2), (p0, p1, p2) = self.place(j)
            if stage in (5, 6):
                for w, k in enumerate((1, 3, 2)):
                    if stage == 5:
                        put(j, w, d2, self.q2.at[s, j, at(p2, k)], self.r5.at[s, j, w])
                    else:
                        put(j, w, d2, self.g3.at[gs, j, p2], self.g3.at[gs, j, p2])
                continue
            for w in range(2):
                back = 3 - 2 * w
                if stage == 1:
                    put(j, w, d0, self.blk.at[bs, j, pl.ds(at(p0, 2) * 14 + 7 * w, 7)], self.r1.at[s, j, w])
                elif stage == 2:
                    put(j, w, d0, self.c2.at[j, w], self.r2.at[s, j, w])
                elif stage == 3:
                    put(j, w, d1, self.q1.at[s, j, pl.ds(at(p1, 2) * 7 + 4 * w, 4 - w)], (self.r3b if w else self.r3a).at[s, j])
                elif stage == 4:
                    put(j, w, d1, self.c4.at[j, w], self.r4.at[s, j, w])
                else:
                    if stage == 7:
                        start, n = p0 * 28 + p1 * 7, 7
                    elif stage == 8:
                        start, n = p0 * 28 + at(p1, back) * 7 + 4 * w, 4 - w
                    elif stage == 9:
                        start, n = p0 * 28, 28
                    else:
                        start, n = at(p0, back) * 28 + 14 * w, 14
                    part = self.whole.at[ws, j, pl.ds(start, n)]
                    put(j, w, d0 if stage > 8 else d1, part, part)
        return out

    def math(self, stage, b):
        s, bs, gs, ws = lax.rem(b, 2), lax.rem(b, NS), lax.rem(b, NG), lax.rem(b, NL)
        for j in range(3):
            _, (p0, p1, p2) = self.place(j)
            if stage == 2:

                def own(k, half):
                    return self.blk[bs, j, pl.ds(at(p0, k) * 14 + 7 * half, 7)].reshape(14, 16, 128)

                def came(w):
                    return self.r1[s, j, w].reshape(14, 16, 128)

                self.c2[j, 0, 0:14] = add(own(1, 0), came(0)).astype(bf16)
                self.c2[j, 0, 14:28] = own(1, 1)
                self.c2[j, 1, 0:14] = own(3, 0)
                self.c2[j, 1, 14:28] = add(own(3, 1), came(1)).astype(bf16)
            elif stage == 3:
                mine = self.blk[bs, j, pl.ds(p0 * 14, 14)].reshape(28, 16, 128)
                self.q1[s, j] = add(mine, self.r2[s, j, 0], self.r2[s, j, 1]).astype(bf16)
            elif stage == 4:

                def own(k, start, n):
                    return self.q1[s, j, pl.ds(at(p1, k) * 7 + start, n)]

                self.c4[j, 0, 0:4] = add(own(1, 0, 4), self.r3a[s, j]).astype(bf16)
                self.c4[j, 0, 4:7] = own(1, 4, 3)
                self.c4[j, 1, 0:4] = own(3, 0, 4)
                self.c4[j, 1, 4:7] = add(own(3, 4, 3), self.r3b[s, j]).astype(bf16)
            elif stage == 5:
                total = add(self.q1[s, j, pl.ds(p1 * 7, 7)], self.r4[s, j, 0], self.r4[s, j, 1]).reshape(14, 8, 128)
                for k, start in enumerate(START):
                    self.q2[s, j, k] = total[start : start + 4].reshape(2, 16, 128).astype(bf16)
            elif stage == 6:
                g = add(self.q2[s, j, p2], *(self.r5[s, j, w] for w in range(3))).astype(bf16)
                self.g3[gs, j, p2] = g
                square = g.astype(f32).reshape(4, 8, 128)
                square = square * square
                self.ssq[...] += square[0] * jnp.where(lax.rem(p2, 2) == 1, 0.0, 1.0) + square[1] + square[2] + square[3]
            elif stage == 7:
                g = self.g3[gs, j].astype(f32).reshape(4, 4, 8, 128)
                g = jnp.concatenate([g[0], g[1, 1:], g[2], g[3, 1:]], axis=0)
                self.whole[ws, j, pl.ds(p0 * 28 + p1 * 7, 7)] = g.reshape(7, 16, 128).astype(bf16)

    def out(self, b):
        return pltpu.make_async_copy(self.whole.at[lax.rem(b, NL)], self.g_hbm.at[b], self.osem.at[lax.rem(b, 2)])

    def stage(self, k, b):
        if 2 <= k <= 11:
            for c in self.copies(k - 1, b):
                c.wait()
        if k <= 10:
            self.math(k, b)
            for c in self.copies(k, b):
                c.start()
        elif k == 11:
            self.out(b).start()
        else:
            self.out(b).wait()

    def due(self, tick, low, high):
        for k in range(high, low - 1, -1):
            u = tick - k
            late = u >= ready(NB)
            now = (u >= ready(0)) & (u <= END) & (late | (lax.rem(u, 2) == 1))
            pl.when(now)(functools.partial(self.stage, k, jnp.where(late, u - NB, lax.div(u, 2))))

    def scatter(self, tick):
        self.due(tick, 1, SUMMED)

    def gather(self, tick):
        self.due(tick, SUMMED + 1, LAST)

    def total(self, step):
        def copy(step):
            d, odd = divmod(step, 2)
            peer = jnp.where(lax.rem(self.pos[d], 2) == odd, *self.near[d][:2])
            return pltpu.make_async_remote_copy(
                src_ref=self.ssq_to.at[step],
                dst_ref=self.ssq_from.at[step],
                send_sem=self.qsend.at[step],
                recv_sem=self.qrecv.at[step],
                device_id={"dp": peer},
                device_id_type=MESH,
            )

        if step > 0:
            copy(step - 1).wait()
            self.ssq[...] += self.ssq_from[step - 1]
        if step < 6:
            self.ssq_to[step] = self.ssq[...]
            copy(step).start()


def backward(names, h1_hbm, dy_hbm, a0t_hbm, s_hbm, a_hbm, act_hbm, a1_hbm, a1t_hbm, dyt_hbm, wg, wu, wd, g_hbm, ssq_out, *scratch):
    refs = dict(zip(names, scratch, strict=True))
    h1, dy, a, a_t, dy_t, da, wgu, wdb, act, dgu, sb, ab, isem, wsem = (refs.pop(n) for n in OWN)
    comm = Comm(refs, g_hbm)
    first = [
        pltpu.make_async_copy(src, dst, isem.at[k]) for k, (src, dst) in enumerate(((a1_hbm, a), (dy_hbm, dy), (a1t_hbm, a_t), (dyt_hbm, dy_t), (h1_hbm, h1)))
    ]

    def fetch1(b, slot):
        return (
            pltpu.make_async_copy(wg.at[1, :, block(b)], wgu.at[slot, :, 0:FB], wsem.at[slot, 0]),
            pltpu.make_async_copy(wu.at[1, :, block(b)], wgu.at[slot, :, FB : 2 * FB], wsem.at[slot, 1]),
            pltpu.make_async_copy(wd.at[1, block(b), :], wdb.at[slot], wsem.at[slot, 2]),
        )

    def fetch0(b, slot):
        return (
            pltpu.make_async_copy(s_hbm.at[b], sb.at[slot], wsem.at[slot, 0]),
            pltpu.make_async_copy(a_hbm.at[b], ab.at[slot], wsem.at[slot, 1]),
            pltpu.make_async_copy(act_hbm.at[:, block(b)], act.at[slot], wsem.at[slot, 3]),
            pltpu.make_async_copy(wd.at[0, block(b), :], wdb.at[slot], wsem.at[slot, 2]),
        )

    for c in fetch1(0, 0):
        c.start()
    for c in first:
        c.start()

    @pl.loop(0, T // TM)
    def _(t):
        da[rows(t), :] = jnp.zeros((TM, D), f32)

    comm.barrier()
    for c in first:
        c.wait()

    def give(slot, j, g):
        for half in range(2):
            comm.blk[slot, j, :, half] = g[:, half * 128 : (half + 1) * 128].astype(bf16).reshape(56, 16, 128)

    @pl.loop(0, NB)
    def _(b):
        slot, to = lax.rem(b, 2), lax.rem(b, NS)

        def tokens(tiles):
            for t in tiles:
                r = pl.ds(t * TM, TM)
                both = dot(a[r, :], wgu[slot])
                gate, up = both[:, :FB], both[:, FB:]
                dact = dot_t(dy[r, :], wdb[slot]).astype(bf16).astype(f32)
                sg = 1.0 / (1.0 + jnp.exp(-gate))
                s = gate * sg
                act[0, r, :] = (s * up).astype(bf16)
                dgu[r, :FB] = (dact * up * (sg + s * (1.0 - sg))).astype(bf16)
                dgu[r, FB:] = (dact * s).astype(bf16)
                da[r, :] += dot_t(dgu[r, :], wgu[slot])

        comm.scatter(2 * b)

        @pl.when(b + 1 < NB)
        def _():
            for c in fetch1(b + 1, 1 - slot):
                c.start()

        for c in fetch1(b, slot):
            c.wait()
        tokens(range(0, T // TM // 2))
        comm.gather(2 * b)
        tokens(range(T // TM // 2, T // TM))
        comm.scatter(2 * b + 1)
        both = dot(a_t[...], dgu[...])
        give(to, 0, both[:, :FB])
        give(to, 1, both[:, FB:])
        comm.gather(2 * b + 1)
        give(to, 2, dot(dy_t[...], act[0]))

    for c in fetch0(0, 0):
        c.start()
    last = pltpu.make_async_copy(a0t_hbm, a_t, isem.at[0])
    last.start()

    @pl.loop(0, T // TM)
    def _(t):
        h = h1[rows(t), :].astype(f32)
        scale = norm_scale(h)
        g = da[rows(t), :].astype(bf16).astype(f32)
        along = jnp.mean(g * h, -1, keepdims=True)
        dh = (g * scale - h * (scale * scale * scale * along)).astype(bf16) + dy[rows(t), :]
        dy[rows(t), :] = dh
        dy_t[:, rows(t)] = dh.T

    last.wait()

    @pl.loop(0, NB)
    def _(b):
        tick = b + 2 * NB
        comm.scatter(tick)
        slot, to = lax.rem(b, 2), lax.rem(b + NB, NS)

        @pl.when(b + 1 < NB)
        def _():
            for c in fetch0(b + 1, 1 - slot):
                c.start()

        for c in fetch0(b, slot):
            c.wait()
        for t in range(T // TM):
            r = pl.ds(t * TM, TM)
            dact = dot_t(dy[r, :], wdb[slot]).astype(bf16).astype(f32)
            dgu[r, :FB] = (dact * ab[slot, r, :]).astype(bf16)
            dgu[r, FB:] = (dact * sb[slot, r, :]).astype(bf16)
        give(to, 2, dot(dy_t[...], act[slot]))
        comm.gather(tick)
        both = dot(a_t[...], dgu[...])
        give(to, 0, both[:, :FB])
        give(to, 1, both[:, FB:])

    @pl.loop(END + 1, END + LAST + 1)
    def _(tick):
        comm.scatter(tick)
        comm.gather(tick)
        for step in range(7):
            pl.when(tick == END + SUMMED + step)(functools.partial(comm.total, step))

    ssq_out[...] = comm.ssq[...]


OWN = ("h1", "dy", "a", "a_t", "dy_t", "da", "wgu", "wdb", "act", "dgu", "sb", "ab", "isem", "wsem")


def run_backward(*args):
    own = dict(
        h1=pltpu.VMEM((T, D), bf16),
        dy=pltpu.VMEM((T, D), bf16),
        a=pltpu.VMEM((T, D), bf16),
        a_t=pltpu.VMEM((D, T), bf16),
        dy_t=pltpu.VMEM((D, T), bf16),
        da=pltpu.VMEM((T, D), f32),
        wgu=pltpu.VMEM((2, D, 2 * FB), bf16),
        wdb=pltpu.VMEM((2, FB, D), bf16),
        act=pltpu.VMEM((2, T, FB), bf16),
        dgu=pltpu.VMEM((T, 2 * FB), bf16),
        sb=pltpu.VMEM((2, T, FB), f32),
        ab=pltpu.VMEM((2, T, FB), f32),
        isem=pltpu.SemaphoreType.DMA((5,)),
        wsem=pltpu.SemaphoreType.DMA((2, 4)),
    )
    scratch = own | comm_scratch()
    return pl.pallas_call(
        functools.partial(backward, tuple(scratch)),
        name="backward",
        out_shape=(sds((NBLK, 3, 112, 16, 128), bf16), sds((8, 128), f32)),
        in_specs=[ANY] * 12,
        out_specs=(ANY, VMEM),
        scratch_shapes=list(scratch.values()),
        compiler_params=pltpu.CompilerParams(collective_id=0, has_side_effects=True, vmem_limit_bytes=VMEM_LIMIT),
    )(*args)


def adamw(ssq_ref, g_ref, *refs):
    factor = jnp.minimum(1.0, 0.5 * lax.rsqrt(jnp.sum(ssq_ref[...], keepdims=True) / COUNT + 1e-30))
    ins, outs = refs[:9], refs[9:]

    @pl.loop(0, NB)
    def _(b):
        for k in range(3):
            tiles = g_ref[b, k].reshape(8, 2, 16, 128)
            for half in range(2):
                g = tiles[:, half].reshape(128, 128)
                units = pl.ds(pl.multiple_of(b * FB + half * 128, 128), 128)
                where = (0, slice(None), units)
                if k == 2:
                    g, where = g.T, (0, units, slice(None))
                w, m, v = (ins[i + k][where].astype(f32) for i in (0, 3, 6))
                g = g.astype(f32) * factor
                m = 0.9 * m + 0.1 * g
                v = 0.95 * v + 0.05 * g * g
                step = m * lax.rsqrt(v + 1e-8) + 0.1 * w
                outs[k][where] = (w - 0.02 * step).astype(bf16)
                outs[3 + k][where] = m
                outs[6 + k][where] = v


def run_adamw(ssq, g, *arrays):
    wide = pl.BlockSpec((1, 128, F), lambda n, i: (1 - n, i, 0))
    tall = pl.BlockSpec((1, F, 128), lambda n, i: (1 - n, 0, i))
    specs = [wide, wide, tall] * 3
    return pl.pallas_call(
        adamw,
        name="adamw",
        grid=(LAYERS, D // 128),
        out_shape=tuple(sds(a.shape, a.dtype) for a in arrays),
        in_specs=[pl.BlockSpec((8, 128), lambda n, i: (0, 0)), pl.BlockSpec((NB, 3, 16, 16, 128), lambda n, i: (n, 0, i, 0, 0))] + specs,
        out_specs=tuple(specs),
        compiler_params=pltpu.CompilerParams(vmem_limit_bytes=VMEM_LIMIT, dimension_semantics=("arbitrary", "arbitrary")),
    )(ssq, g, *arrays)


def solution(mesh):
    def step(x, dy, *arrays):
        wg, wu, wd = arrays[:3]
        s, a, act, h1, a0t, a1, a1t, dyt = run_forward(x[0], dy[0], wg, wu, wd)
        g, ssq = run_backward(h1, dy[0], a0t, s, a, act, a1, a1t, dyt, wg, wu, wd)
        return run_adamw(ssq, g, *arrays)

    return jax.shard_map(
        step,
        mesh=mesh,
        in_specs=(P(("rep", "dp"), None, None),) * 2 + (P(None, None, None),) * 9,
        out_specs=(P("rep", None, None),) * 9,
        check_vma=False,
    )
```

time: 423 us -> 408 us (0.965)
  Pallas kernels: 422 us -> 407 us
    pallas_call x1, Pallas kernels: 285 us -> 272 us  [run_backward(): pl.pallas_call(functools.partial(backward, tuple(scratch)), name='backwar...]
    pallas_call x1, Pallas kernels: 96.6 us -> 89.4 us  [run_adamw(): pl.pallas_call(adamw, name='adamw', grid=(LAYERS, D // 128), out_shape=tu...]
    pallas_call x1, Pallas kernels: 41.1 us -> 45.4 us  [run_forward(): pl.pallas_call(forward, name='forward', out_shape=(sds((NB, T, FB), f32),...]
where the time goes in v2:
time: 408 us
  Pallas kernels  407 us (100%)
    pallas_call x1, Pallas kernels, run_backward(): pl.pallas_call(functools.partial(backward, tuple(scratch)), name='backwar...  272 us
    pallas_call x1, Pallas kernels, run_adamw(): pl.pallas_call(adamw, name='adamw', grid=(LAYERS, D // 128), out_shape=tu...  89.4 us
    pallas_call x1, Pallas kernels, run_forward(): pl.pallas_call(forward, name='forward', out_shape=(sds((NB, T, FB), f32),...  45.4 us

profile of v2, /device:TPU:0, one launch (start us, length us, event | category | flops | bytes accessed | tf_op | source)
XLA Modules:
  0.0 408.0 jit_solution(1592605147712427369)
XLA Ops:
  0.6 45.4 %forward.1 = (f32[9,2048,256]{2,1,0:T(8,128)}, f32[9,2048,256]{2,1,0:T(8,128)}, bf16[2048,2304]{1,0:T(8,128)(2,1)}, bf16[2048,896]{1,0:T(8,128)(2,1)}, bf16[896,...) custom-call(bf16[2048,896]{1,0:T(8,128)(2,1)} %bitcast.4, ...), custom_call_target="tpu_custom_call" | custom-call | tf_op jit(solution)/shard_map/forward/pallas_call | solution.py:140
  46.0 272.3 %backward.1 = (bf16[18,3,112,16,128]{4,3,2,1,0:T(8,128)(2,1)}, f32[8,128]{1,0:T(8,128)}) custom-call(bf16[2048,896]{1,0:T(8,128)(2,1)} %get-tuple-element.19.h1_hbm, bf16[2048,896]{1,0:T(8,128)(2,1)} %bitcast.3, bf16[896,2048]{1,0:T(8,128)(2,1)} %get-tuple-element.20.a0t_hbm, f32[9,2048,256]{2,1,0:T(8,128)} %get-tuple-element.21.s_hbm, ...), custom_call_target="tpu_custom_call" | custom-call | tf_op jit(solution)/shard_map/backward/pallas_call | solution.py:523
  318.4 89.4 %adamw.1 = (bf16[2,896,2304]{2,1,0:T(8,128)(2,1)}, bf16[2,896,2304]{2,1,0:T(8,128)(2,1)}, bf16[2,2304,896]{2,1,0:T(8,128)(2,1)}, f32[2,896,2304]{2,1,0:T(8,128)}...) custom-call(f32[8,128]{1,0:T(8,128)} %get-tuple-element.27.ssq_ref, ...), custom_call_target="tpu_custom_call" | custom-call | tf_op jit(solution)/shard_map/adamw/pallas_call | solution.py:562
